TPU v7x, 32 devices: a whole 2x2x4 slice. The times are simulated.
32 devices in a mesh: row: 8 (over z, y), col: 4 (over x, core).
Axes of the slice: x: 2, y: 2, z: 4, core: 2. Of those that a mesh axis runs over, the one named last changes fastest.
Arguments:
- matrix: float32 [4096, 4096], P('row', 'col'), may hold values from -0.92 to 1.92, as said below
Outputs:
- inverse: float32 [4096, 4096], P('row', 'col')
- residual_norms: float32 [4], replicated
Inputs may be any that keep to these rules, and one draw needn't show every extreme that they name: matrix is exactly symmetric and positive definite; all its eigenvalues lie between 0.08 and 1.92.
All inputs are finite; a program needn't handle non-finite values.
Results may differ from a plain program's by a relative error of at most 0.0017.
The roundings to bfloat16 on the way count: a program that leaves them out, or rounds other values in their place, can miss the bound.
Values may be sent and summed in bfloat16 or wider, within the bound.
A program may use at most 64 MiB of HBM per device.

v0:
```python
import jax
import jax.numpy as jnp
from jax import lax
from jax.sharding import PartitionSpec as P

N = 4096
ITERS = 4


def shards(matrix):
    row_count, col_count = matrix.shape
    row_index = lax.axis_index("row")
    col_index = lax.axis_index("col")
    sq_total = lax.psum(jnp.sum(matrix * matrix), ("row", "col"))
    start_scale = jnp.sqrt(jnp.float32(N)) / jnp.sqrt(sq_total)
    global_rows = row_index * row_count + lax.broadcasted_iota(jnp.int32, (row_count, col_count), 0)
    global_cols = col_index * col_count + lax.broadcasted_iota(jnp.int32, (row_count, col_count), 1)
    eye_block = (global_rows == global_cols).astype(jnp.float32)
    mat_low = matrix.astype(jnp.bfloat16)
    panel_rows = lax.all_gather(mat_low, "col", axis=1, tiled=True)
    current = start_scale * eye_block
    partial_list = []
    for iteration in range(ITERS):
        cur_low = current.astype(jnp.bfloat16)
        product = jnp.dot(
            panel_rows,
            lax.all_gather(cur_low, "row", axis=0, tiled=True),
            preferred_element_type=jnp.float32,
        )
        residual = eye_block - product
        local_sum = jnp.sum(residual * residual)
        partial_list.append(local_sum)
        shift_low = (eye_block + residual).astype(jnp.bfloat16)
        iterate_rows = lax.all_gather(cur_low, "col", axis=1, tiled=True)
        current = jnp.dot(
            iterate_rows,
            lax.all_gather(shift_low, "row", axis=0, tiled=True),
            preferred_element_type=jnp.float32,
        )
    summed = lax.psum(jnp.stack(partial_list), ("row", "col"))
    residual_norms = jnp.sqrt(summed / N)
    return (current, residual_norms)


def solution(mesh):
    in_specs = (P("row", "col"),)
    out_specs = (P("row", "col"), P())
    return jax.shard_map(shards, mesh=mesh, in_specs=in_specs, out_specs=out_specs, check_vma=False)
```

profile of v0, /device:TPU:0, one launch (start us, length us, event | category | flops | bytes accessed | tf_op | source)
XLA Modules:
  0.0 1244.2 jit_solution(14768718448786911574)
XLA Ops:
  7.2 4.3 fusion.5
  11.6 42.5 %psum.14 = f32[]{:T(128)} all-reduce(f32[]{:T(128)} %get-tuple-element.8), channel_id=1, replica_groups=mesh['row'=8,'col'=4] {'row','col'}, use_global_device_ids=true, to_apply=%region_1.0 | all-reduce | flops 1 | bytes 8 | tf_op jit(solution)/shard_map/psum | solution.py:14
  54.8 1.2 fusion
  56.1 0.7 all-gather.14.cloned.1.call-update
  56.9 124.6 %all-gather.16.cloned.1.call-done = bf16[4096,1024]{0,1:T(8,128)(2,1)} async-done(((bf16[512,1024]{0,1:T(8,128)(2,1)}), bf16[4096,1024]{0,1:T(8,128)(2,1)}) %all-gather.16.cloned.1.call-update) | async-done | bytes 8388624 | tf_op jit(solution)/shard_map/all_gather | solution.py:27
  181.5 10.1 fusion.1
  191.7 24.1 %all-gather.14.cloned.1.call-done = bf16[512,4096]{0,1:T(8,128)(2,1)} async-done(((bf16[512,1024]{0,1:T(8,128)(2,1)}), bf16[512,4096]{0,1:T(8,128)(2,1)}) %all-gather.14.cloned.1.call-update) | async-done | bytes 4194320 | tf_op jit(solution)/shard_map/all_gather | solution.py:34
  215.7 127.4 %all-gather.20.cloned.1.call-done = bf16[4096,1024]{0,1:T(8,128)(2,1)} async-done(((bf16[512,1024]{0,1:T(8,128)(2,1)}), bf16[4096,1024]{0,1:T(8,128)(2,1)}) %all-gather.20.cloned.1.call-update) | async-done | bytes 8388624 | tf_op jit(solution)/shard_map/all_gather | solution.py:37
  343.2 10.2 convolution_convert_fusion.2
  353.4 0.5 all-gather.22.cloned.1.call-update
  354.0 0.5 all-gather.26.cloned.1.call-start
  354.5 121.7 %all-gather.24.cloned.1.call-done = bf16[4096,1024]{1,0:T(8,128)(2,1)} async-done(((bf16[512,1024]{1,0:T(8,128)(2,1)}), bf16[4096,1024]{1,0:T(8,128)(2,1)}) %all-gather.24.cloned.1.call-update) | async-done | bytes 8388624 | tf_op jit(solution)/shard_map/all_gather | solution.py:27
  476.2 10.9 fusion.2
  487.1 23.1 %all-gather.22.cloned.1.call-done = bf16[512,4096]{1,0:T(8,128)(2,1)} async-done(((bf16[512,1024]{1,0:T(8,128)(2,1)}), bf16[512,4096]{1,0:T(8,128)(2,1)}) %all-gather.22.cloned.1.call-update) | async-done | bytes 4194320 | tf_op jit(solution)/shard_map/all_gather | solution.py:34
  510.3 127.0 %all-gather.26.cloned.1.call-done = bf16[4096,1024]{0,1:T(8,128)(2,1)} async-done(((bf16[512,1024]{0,1:T(8,128)(2,1)}), bf16[4096,1024]{0,1:T(8,128)(2,1)}) %all-gather.26.cloned.1.call-update) | async-done | bytes 8388624 | tf_op jit(solution)/shard_map/all_gather | solution.py:37
  637.3 10.2 convolution_convert_fusion.1
  647.5 0.7 all-gather.28.cloned.1.call-update
  648.2 0.2 all-gather.32.cloned.1.call-start
  648.4 121.9 %all-gather.30.cloned.1.call-done = bf16[4096,1024]{1,0:T(8,128)(2,1)} async-done(((bf16[512,1024]{1,0:T(8,128)(2,1)}), bf16[4096,1024]{1,0:T(8,128)(2,1)}) %all-gather.30.cloned.1.call-update) | async-done | bytes 8388624 | tf_op jit(solution)/shard_map/all_gather | solution.py:27
  770.3 10.9 fusion.3
  781.2 23.3 %all-gather.28.cloned.1.call-done = bf16[512,4096]{1,0:T(8,128)(2,1)} async-done(((bf16[512,1024]{1,0:T(8,128)(2,1)}), bf16[512,4096]{1,0:T(8,128)(2,1)}) %all-gather.28.cloned.1.call-update) | async-done | bytes 4194320 | tf_op jit(solution)/shard_map/all_gather | solution.py:34
  804.5 126.9 %all-gather.32.cloned.1.call-done = bf16[4096,1024]{0,1:T(8,128)(2,1)} async-done(((bf16[512,1024]{0,1:T(8,128)(2,1)}), bf16[4096,1024]{0,1:T(8,128)(2,1)}) %all-gather.32.cloned.1.call-update) | async-done | bytes 8388624 | tf_op jit(solution)/shard_map/all_gather | solution.py:37
  931.4 10.2 convolution_convert_fusion
  941.6 0.5 all-gather.34.cloned.1.call-update
  942.2 0.3 all-gather.38.cloned.1.call-start
  942.4 122.0 %all-gather.36.cloned.1.call-done = bf16[4096,1024]{1,0:T(8,128)(2,1)} async-done(((bf16[512,1024]{1,0:T(8,128)(2,1)}), bf16[4096,1024]{1,0:T(8,128)(2,1)}) %all-gather.36.cloned.1.call-update) | async-done | bytes 8388624 | tf_op jit(solution)/shard_map/all_gather | solution.py:27
  1064.4 12.9 %multiply_reduce_fusion.3 = (f32[]{:T(128)}, f32[]{:T(128)}, f32[]{:T(128)}, f32[]{:T(128)}, bf16[512,1024]{0,1:T(8,128)(2,1)}) fusion(f32[1024,512]{1,0:T(8,128)S(1)} %get-tuple-element.10, s32[512]{0:T(512)S(1)} %iota_add_fusion.1, s32[1024]{0:T(1024)S(1)} %iota_add_fusion, f32[1024,512]{1,0:T(8,128)} %get-tuple-element.12, ...), kind=kOutput, calls=%fused_computation.17 | convolution fusion | flops 4303355904 | bytes 19929104 | tf_op jit(solution)/shard_map/dot_general | solution.py:25
  1077.4 2.6 pad_maximum_fusion
  1079.9 39.1 %psum.15 = f32[4]{0:T(128)S(1)} all-reduce(f32[4]{0:T(128)S(1)} %pad_maximum_fusion), channel_id=1, replica_groups=mesh['row'=8,'col'=4] {'row','col'}, use_global_device_ids=true, to_apply=%region_6.0 | all-reduce | flops 4 | bytes 32 | tf_op jit(solution)/shard_map/psum | solution.py:40
  1119.1 0.5 multiply_sqrt_fusion
  1119.6 107.3 %all-gather.38.cloned.1.call-done = bf16[4096,1024]{0,1:T(8,128)(2,1)} async-done(((bf16[512,1024]{0,1:T(8,128)(2,1)}), bf16[4096,1024]{0,1:T(8,128)(2,1)}) %all-gather.38.cloned.1.call-update) | async-done | bytes 8388624 | tf_op jit(solution)/shard_map/all_gather | solution.py:37
  1226.9 10.5 fusion.6
  (23 shorter events, 0.6 us)
Async XLA Ops:
  7.2 49.7 %all-gather.18.cloned.1.call-start = ((), (), s32[]{:S(2)}) async-start(), calls=%async_computation.2 | async-start | bytes 5242880 | tf_op jit(solution)/shard_map/all_gather | solution.py:20
  11.5 170.0 %all-gather.16.cloned.1.call-start = ((), (), s32[]{:S(2)}) async-start(), calls=%async_computation.1 | async-start | bytes 9437184 | tf_op jit(solution)/shard_map/all_gather | solution.py:27
  56.1 159.7 %all-gather.14.cloned.1.call-start = ((), (), s32[]{:S(2)}) async-start(), calls=%async_computation | async-start | bytes 5242880 | tf_op jit(solution)/shard_map/all_gather | solution.py:34
  56.8 286.4 %all-gather.20.cloned.1.call-start = ((), (), s32[]{:S(2)}) async-start(), calls=%async_computation.3 | async-start | bytes 9437184 | tf_op jit(solution)/shard_map/all_gather | solution.py:37
  191.6 284.6 %all-gather.24.cloned.1.call-start = ((), (), s32[]{:S(2)}) async-start(), calls=%async_computation.5 | async-start | bytes 9437184 | tf_op jit(solution)/shard_map/all_gather | solution.py:27
  353.4 156.9 %all-gather.22.cloned.1.call-start = ((), (), s32[]{:S(2)}) async-start(), calls=%async_computation.4 | async-start | bytes 5242880 | tf_op jit(solution)/shard_map/all_gather | solution.py:34
  354.0 283.3 %all-gather.26.cloned.1.call-start = ((), (), s32[]{:S(2)}) async-start(), calls=%async_computation.6 | async-start | bytes 9437184 | tf_op jit(solution)/shard_map/all_gather | solution.py:37
  487.1 283.2 %all-gather.30.cloned.1.call-start = ((), (), s32[]{:S(2)}) async-start(), calls=%async_computation.8 | async-start | bytes 9437184 | tf_op jit(solution)/shard_map/all_gather | solution.py:27
  647.5 157.0 %all-gather.28.cloned.1.call-start = ((), (), s32[]{:S(2)}) async-start(), calls=%async_computation.7 | async-start | bytes 5242880 | tf_op jit(solution)/shard_map/all_gather | solution.py:34
  648.2 283.2 %all-gather.32.cloned.1.call-start = ((), (), s32[]{:S(2)}) async-start(), calls=%async_computation.9 | async-start | bytes 9437184 | tf_op jit(solution)/shard_map/all_gather | solution.py:37
  781.2 283.2 %all-gather.36.cloned.1.call-start = ((), (), s32[]{:S(2)}) async-start(), calls=%async_computation.11 | async-start | bytes 9437184 | tf_op jit(solution)/shard_map/all_gather | solution.py:27
  941.6 178.0 %all-gather.34.cloned.1.call-start = ((), (), s32[]{:S(2)}) async-start(), calls=%async_computation.10 | async-start | bytes 5242880 | tf_op jit(solution)/shard_map/all_gather | solution.py:34
  942.2 284.7 %all-gather.38.cloned.1.call-start = ((), (), s32[]{:S(2)}) async-start(), calls=%async_computation.12 | async-start | bytes 9437184 | tf_op jit(solution)/shard_map/all_gather | solution.py:37
Sparse Core Ops, SparseCore 0:
  11.6 37.4 all-gather.17
  56.2 125.2 all-gather.15
  183.1 32.6 all-gather.13
  218.2 124.9 all-gather.19
  353.5 122.6 all-gather.23
  477.6 32.6 all-gather.21
  512.3 124.9 all-gather.25
  647.6 122.6 all-gather.29
  771.9 32.6 all-gather.27
  806.4 124.9 all-gather.31
  941.7 122.6 all-gather.35
  1065.8 33.3 all-gather.33
  1101.2 125.6 all-gather.37
where the time goes:
time: 1250 us; the launch traced here: 1240 us
  waiting for transfers between devices  1050 us (84%)
  matrix products  85.8 us (7%)
  blocking collectives  81.7 us (7%)
  between operations  14.9 us (1%)
    all_gather x4, waiting for transfers between devices, shards(): lax.all_gather(cur_low, 'row', axis=0, tiled=True)  490 us
    all_gather x4, waiting for transfers between devices, shards(): lax.all_gather(shift_low, 'row', axis=0, tiled=True)  489 us
    all_gather x4, waiting for transfers between devices, shards(): iterate_rows = lax.all_gather(cur_low, 'col', axis=1, tiled=True)  70.5 us
    dot_general x4, matrix products, shards(): jnp.dot(panel_rows, lax.all_gather(cur_low, 'row', axis=0, tiled=True), p...  44.8 us
    psum x1, blocking collectives, shards(): sq_total = lax.psum(jnp.sum(matrix * matrix), ('row', 'col'))  42.5 us
    dot_general x4, matrix products, shards(): jnp.dot(iterate_rows, lax.all_gather(shift_low, 'row', axis=0, tiled=True...  41 us
    psum x1, blocking collectives, shards(): summed = lax.psum(jnp.stack(partial_list), ('row', 'col'))  39.1 us
  transfers between devices with their start and end apart: 13, of which 11 were waited for; matrix products, arithmetic and copies ran while one was open for 4% of the time, Pallas kernels for 0%

commit v1 on v0

--- a/solution.py
+++ b/solution.py
@@ -32,10 +32,14 @@
         partial_list.append(local_sum)
         shift_low = (eye_block + residual).astype(jnp.bfloat16)
         iterate_rows = lax.all_gather(cur_low, "col", axis=1, tiled=True)
+
+        def wait_field(v0, across):
+            w2 = jnp.stack([v0 for _ in range(jax.lax.axis_size(across))])
+            view_out = jax.lax.all_to_all(w2, across, 0, 0)
+            return jnp.concatenate(view_out, axis=0)
+
         current = jnp.dot(
-            iterate_rows,
-            lax.all_gather(shift_low, "row", axis=0, tiled=True),
-            preferred_element_type=jnp.float32,
+            iterate_rows, wait_field(shift_low, "row"), preferred_element_type=jnp.float32
         )
     summed = lax.psum(jnp.stack(partial_list), ("row", "col"))
     residual_norms = jnp.sqrt(summed / N)

time: 1250 us -> 1440 us (1.15)
  blocking collectives: 81.7 us -> 242 us
  starting transfers between devices: 1.37 us -> 21.2 us
  local copies, waits for them, and re-layouts: 0 us -> 19.4 us
    all_gather x4 -> x0, waiting for transfers between devices: 489 us -> none  [shards(): lax.all_gather(shift_low, 'row', axis=0, tiled=True)]
    all_to_all x0 -> x4, waiting for transfers between devices: none -> 434 us  [wait_field(): view_out = jax.lax.all_to_all(w2, across, 0, 0)]
    psum x1, blocking collectives: 39.1 us -> 199 us  [shards(): summed = lax.psum(jnp.stack(partial_list), ('row', 'col'))]
    all_gather x4, waiting for transfers between devices: 70.5 us -> 111 us  [shards(): iterate_rows = lax.all_gather(cur_low, 'col', axis=1, tiled=True)]
    all_to_all x0 -> x4, starting transfers between devices: none -> 19.8 us  [wait_field(): view_out = jax.lax.all_to_all(w2, across, 0, 0)]
    another operation x0 -> x4, local copies, waits for them, and re-layouts: none -> 17.3 us  [wait_field(): w2 = jnp.stack([v0 for _ in range(jax.lax.axis_size(across))])]
  transfers between devices with their start and end apart: 13 -> 13, of which waited for: 11 -> 10; matrix products, arithmetic and copies ran while one was open for 4% -> 0% of each run, Pallas kernels for 0% -> 0%
where the time goes in v1:
time: 1440 us; the launch traced here: 1430 us
  waiting for transfers between devices  1040 us (72%)
  blocking collectives  242 us (17%)
  matrix products  84.9 us (6%)
  starting transfers between devices  21.2 us (1%)
  local copies, waits for them, and re-layouts  19.4 us (1%)
  between operations  14.9 us (1%)
    all_gather x4, waiting for transfers between devices, shards(): lax.all_gather(cur_low, 'row', axis=0, tiled=True)  496 us
    all_to_all x4, waiting for transfers between devices, wait_field(): view_out = jax.lax.all_to_all(w2, across, 0, 0)  434 us
    psum x1, blocking collectives, shards(): summed = lax.psum(jnp.stack(partial_list), ('row', 'col'))  199 us
    all_gather x4, waiting for transfers between devices, shards(): iterate_rows = lax.all_gather(cur_low, 'col', axis=1, tiled=True)  111 us
    dot_general x4, matrix products, shards(): jnp.dot(panel_rows, lax.all_gather(cur_low, 'row', axis=0, tiled=True), p...  43.9 us
    psum x1, blocking collectives, shards(): sq_total = lax.psum(jnp.sum(matrix * matrix), ('row', 'col'))  42.5 us
    dot_general x4, matrix products, shards(): jnp.dot(iterate_rows, wait_field(shift_low, 'row'), preferred_element_typ...  41 us
  transfers between devices with their start and end apart: 13, of which 10 were waited for; matrix products, arithmetic and copies ran while one was open for 0% of the time, Pallas kernels for 0%

profile of v1, /device:TPU:0, one launch (start us, length us, event | category | flops | bytes accessed | tf_op | source)
XLA Modules:
  0.0 1434.6 jit_solution(6027263705423390062)
XLA Ops:
  7.2 4.3 fusion.5
  11.6 42.5 %psum.14 = f32[]{:T(128)} all-reduce(f32[]{:T(128)} %get-tuple-element.8), channel_id=1, replica_groups=mesh['row'=8,'col'=4] {'row','col'}, use_global_device_ids=true, to_apply=%region_1.0 | all-reduce | flops 1 | bytes 8 | tf_op jit(solution)/shard_map/psum | solution.py:14
  54.8 1.3 fusion
  56.2 125.4 %all-gather.12.cloned.1.call-done = bf16[4096,1024]{0,1:T(8,128)(2,1)} async-done(((bf16[512,1024]{0,1:T(8,128)(2,1)}), bf16[4096,1024]{0,1:T(8,128)(2,1)}) %all-gather.12.cloned.1.call-update) | async-done | bytes 8388624 | tf_op jit(solution)/shard_map/all_gather | solution.py:27
  181.5 10.4 fusion.1
  192.5 4.3 stack.18
  196.8 5.0 all-to-all-start
  202.8 37.1 %all-gather.10.cloned.1.call-done = bf16[512,4096]{0,1:T(8,128)(2,1)} async-done(((bf16[512,1024]{0,1:T(8,128)(2,1)}), bf16[512,4096]{0,1:T(8,128)(2,1)}) %all-gather.10.cloned.1.call-update) | async-done | bytes 4194320 | tf_op jit(solution)/shard_map/all_gather | solution.py:34
  239.9 144.4 %all-to-all-done = bf16[8,512,1024]{2,1,0:T(8,128)(2,1)} async-done(((bf16[8,512,1024]{2,1,0:T(8,128)(2,1)}), bf16[8,512,1024]{2,1,0:T(8,128)(2,1)}, u32[]{:S(2)}, u32[]{:S(2)}) %all-to-all-start) | async-done | bytes 8388640 | tf_op jit(solution)/shard_map/all_to_all | solution.py:38
  384.3 10.1 convolution_convert_fusion.2
  394.5 123.7 %all-gather.18.cloned.1.call-done = bf16[4096,1024]{1,0:T(8,128)(2,1)} async-done(((bf16[512,1024]{1,0:T(8,128)(2,1)}), bf16[4096,1024]{1,0:T(8,128)(2,1)}) %all-gather.18.cloned.1.call-update) | async-done | bytes 8388624 | tf_op jit(solution)/shard_map/all_gather | solution.py:27
  518.2 10.6 fusion.2
  529.4 4.3 stack.19
  533.7 5.0 all-to-all-start.1
  539.8 36.7 %all-gather.16.cloned.1.call-done = bf16[512,4096]{1,0:T(8,128)(2,1)} async-done(((bf16[512,1024]{1,0:T(8,128)(2,1)}), bf16[512,4096]{1,0:T(8,128)(2,1)}) %all-gather.16.cloned.1.call-update) | async-done | bytes 4194320 | tf_op jit(solution)/shard_map/all_gather | solution.py:34
  576.5 144.8 %all-to-all-done.1 = bf16[8,512,1024]{2,1,0:T(8,128)(2,1)} async-done(((bf16[8,512,1024]{2,1,0:T(8,128)(2,1)}), bf16[8,512,1024]{2,1,0:T(8,128)(2,1)}, u32[]{:S(2)}, u32[]{:S(2)}) %all-to-all-start.1) | async-done | bytes 8388640 | tf_op jit(solution)/shard_map/all_to_all | solution.py:38
  721.3 10.2 convolution_convert_fusion.1
  731.5 123.6 %all-gather.22.cloned.1.call-done = bf16[4096,1024]{1,0:T(8,128)(2,1)} async-done(((bf16[512,1024]{1,0:T(8,128)(2,1)}), bf16[4096,1024]{1,0:T(8,128)(2,1)}) %all-gather.22.cloned.1.call-update) | async-done | bytes 8388624 | tf_op jit(solution)/shard_map/all_gather | solution.py:27
  855.1 10.5 fusion.3
  866.2 4.3 stack.20
  870.5 5.0 all-to-all-start.2
  875.5 0.7 all-gather.20.cloned.1.call-update
  876.4 37.2 %all-gather.20.cloned.1.call-done = bf16[512,4096]{1,0:T(8,128)(2,1)} async-done(((bf16[512,1024]{1,0:T(8,128)(2,1)}), bf16[512,4096]{1,0:T(8,128)(2,1)}) %all-gather.20.cloned.1.call-update) | async-done | bytes 4194320 | tf_op jit(solution)/shard_map/all_gather | solution.py:34
  913.6 144.5 %all-to-all-done.2 = bf16[8,512,1024]{2,1,0:T(8,128)(2,1)} async-done(((bf16[8,512,1024]{2,1,0:T(8,128)(2,1)}), bf16[8,512,1024]{2,1,0:T(8,128)(2,1)}, u32[]{:S(2)}, u32[]{:S(2)}) %all-to-all-start.2) | async-done | bytes 8388640 | tf_op jit(solution)/shard_map/all_to_all | solution.py:38
  1058.1 10.2 convolution_convert_fusion
  1068.3 123.6 %all-gather.26.cloned.1.call-done = bf16[4096,1024]{1,0:T(8,128)(2,1)} async-done(((bf16[512,1024]{1,0:T(8,128)(2,1)}), bf16[4096,1024]{1,0:T(8,128)(2,1)}) %all-gather.26.cloned.1.call-update) | async-done | bytes 8388624 | tf_op jit(solution)/shard_map/all_gather | solution.py:27
  1191.9 12.4 multiply_reduce_fusion.3
  1204.8 4.3 stack.21
  1209.2 5.0 all-to-all-start.3
  1214.8 2.5 pad_maximum_fusion
  1217.4 199.5 %psum.15 = f32[4]{0:T(128)S(1)} all-reduce(f32[4]{0:T(128)S(1)} %pad_maximum_fusion), channel_id=1, replica_groups=mesh['row'=8,'col'=4] {'row','col'}, use_global_device_ids=true, to_apply=%region_6.0 | all-reduce | flops 4 | bytes 32 | tf_op jit(solution)/shard_map/psum | solution.py:44
  1417.4 10.5 fusion.6
  (27 shorter events, 6.0 us)
Async XLA Ops:
  7.2 49.0 %all-gather.14.cloned.1.call-start = ((), (), s32[]{:S(2)}) async-start(), calls=%async_computation.6 | async-start | bytes 5242880 | tf_op jit(solution)/shard_map/all_gather | solution.py:20
  11.5 170.0 %all-gather.12.cloned.1.call-start = ((), (), s32[]{:S(2)}) async-start(), calls=%async_computation.5 | async-start | bytes 9437184 | tf_op jit(solution)/shard_map/all_gather | solution.py:27
  196.8 187.5 %all-to-all-start = ((bf16[8,512,1024]{2,1,0:T(8,128)(2,1)}), bf16[8,512,1024]{2,1,0:T(8,128)(2,1)}, u32[]{:S(2)}, u32[]{:S(2)}) async-start(bf16[8,512,1024]{2,1,0:T(8,128)(2,1)} %stack.18), calls=%async_computation | async-start | bytes 16777216 | tf_op jit(solution)/shard_map/all_to_all | solution.py:38
  201.8 38.2 %all-gather.10.cloned.1.call-start = ((), (), s32[]{:S(2)}) async-start(), calls=%async_computation.4 | async-start | bytes 5242880 | tf_op jit(solution)/shard_map/all_gather | solution.py:34
  202.5 315.7 %all-gather.18.cloned.1.call-start = ((), (), s32[]{:S(2)}) async-start(), calls=%async_computation.8 | async-start | bytes 9437184 | tf_op jit(solution)/shard_map/all_gather | solution.py:27
  533.7 187.6 %all-to-all-start.1 = ((bf16[8,512,1024]{2,1,0:T(8,128)(2,1)}), bf16[8,512,1024]{2,1,0:T(8,128)(2,1)}, u32[]{:S(2)}, u32[]{:S(2)}) async-start(bf16[8,512,1024]{2,1,0:T(8,128)(2,1)} %stack.19), calls=%async_computation.1 | async-start | bytes 16777216 | tf_op jit(solution)/shard_map/all_to_all | solution.py:38
  538.6 37.8 %all-gather.16.cloned.1.call-start = ((), (), s32[]{:S(2)}) async-start(), calls=%async_computation.7 | async-start | bytes 5242880 | tf_op jit(solution)/shard_map/all_gather | solution.py:34
  539.2 315.9 %all-gather.22.cloned.1.call-start = ((), (), s32[]{:S(2)}) async-start(), calls=%async_computation.10 | async-start | bytes 9437184 | tf_op jit(solution)/shard_map/all_gather | solution.py:27
  870.5 187.6 %all-to-all-start.2 = ((bf16[8,512,1024]{2,1,0:T(8,128)(2,1)}), bf16[8,512,1024]{2,1,0:T(8,128)(2,1)}, u32[]{:S(2)}, u32[]{:S(2)}) async-start(bf16[8,512,1024]{2,1,0:T(8,128)(2,1)} %stack.20), calls=%async_computation.2 | async-start | bytes 16777216 | tf_op jit(solution)/shard_map/all_to_all | solution.py:38
  875.5 38.1 %all-gather.20.cloned.1.call-start = ((), (), s32[]{:S(2)}) async-start(), calls=%async_computation.9 | async-start | bytes 5242880 | tf_op jit(solution)/shard_map/all_gather | solution.py:34
  876.2 315.7 %all-gather.26.cloned.1.call-start = ((), (), s32[]{:S(2)}) async-start(), calls=%async_computation.12 | async-start | bytes 9437184 | tf_op jit(solution)/shard_map/all_gather | solution.py:27
  1209.2 208.3 %all-to-all-start.3 = ((bf16[8,512,1024]{2,1,0:T(8,128)(2,1)}), bf16[8,512,1024]{2,1,0:T(8,128)(2,1)}, u32[]{:S(2)}, u32[]{:S(2)}) async-start(bf16[8,512,1024]{2,1,0:T(8,128)(2,1)} %stack.21), calls=%async_computation.3 | async-start | bytes 16777216 | tf_op jit(solution)/shard_map/all_to_all | solution.py:38
  1214.1 203.3 %all-gather.24.cloned.1.call-start = ((), (), s32[]{:S(2)}) async-start(), calls=%async_computation.11 | async-start | bytes 5242880 | tf_op jit(solution)/shard_map/all_gather | solution.py:34
Sparse Core Ops, SparseCore 0:
  11.6 37.4 all-gather.13
  56.2 125.2 all-gather.11
  204.1 35.7 all-gather.9
  394.6 123.5 all-gather.17
  540.7 35.7 all-gather.15
  731.6 123.4 all-gather.21
  877.8 35.7 all-gather.19
  1068.4 123.4 all-gather.25
  1216.5 35.7 all-gather.23
